TPU v7x, 256 devices: a whole 4x4x8 slice. The times are simulated.
256 devices in a mesh: ctx: 32 (over x, z_hi, core), head: 8 (over z_lo, y).
Axes of the slice: x: 4, y: 4, z: 8 (z_hi: 4, z_lo: 2; z = z_hi * 2 + z_lo), core: 2. Of those that a mesh axis runs over, the one named last changes fastest.
Arguments:
- queries: bfloat16 [4096, 64, 576], P('ctx', 'head'), may hold values from -512 to 512
- latents: bfloat16 [4096, 576], P('ctx'), may hold values from -4 to 4
- index_queries: bfloat16 [4096, 64, 128], P('ctx', 'head'), may hold values from -512 to 512
- index_keys: bfloat16 [4096, 128], P('ctx'), may hold values from -4 to 4
- head_weights: float32 [4096, 64], P('ctx', 'head'), may hold values from -1.5 to 1.5
- block_pos: int32 [32], replicated, may hold values from 0 to 31, each once
Outputs:
- grad_index_queries: float32 [4096, 64, 128], P('ctx', 'head')
- grad_index_keys: float32 [4096, 128], P('ctx')
All inputs are finite; a program needn't handle non-finite values.
Results may differ from a plain program's by a relative error of at most 0.008.
Values may be sent and summed in bfloat16 or wider, within the bound.
No kernel may reach another device: no remote copies, remote signals or barrier semaphores. Data moves between devices by JAX's collectives and lax.ppermute only.
A program may use at most 128 MiB of HBM per device.

v0:
```python
import math

import jax
import jax.numpy as jnp
from jax import lax
from jax.experimental import pallas as pl
from jax.experimental.pallas import tpu as pltpu
from jax.sharding import Mesh
from jax.sharding import PartitionSpec as P

SCALE_ATTN = 192.0 ** (-0.5)
LOG2E = math.log2(math.e)
LOSS_SCALE = 1024.0
NEGATIVE = -1e30
KEYS_STEP = 256
F32 = jnp.float32
BF16 = jnp.bfloat16


def nt(a, b):
    return lax.dot_general(a, b, (((1,), (1,)), ((), ())), preferred_element_type=F32)


def nn(a, b):
    return lax.dot_general(a, b, (((1,), (0,)), ((), ())), preferred_element_type=F32)


def kernel(offs_ref, p_ref, iqt_ref, hw_ref, bias_ref, kva_ref, kvb_ref, gq_ref, gka_ref, gkb_ref, s_ref, m_ref, x_ref, t_ref):
    M = p_ref.shape[0]
    R, S = bias_ref.shape
    W = iqt_ref.shape[0]
    heads = M // R
    step = KEYS_STEP
    lanes = step // 128
    tile = 16 * R
    half = kva_ref.shape[0]
    wide = kva_ref.shape[1]
    chunk = half // offs_ref.shape[0]
    qs = SCALE_ATTN * LOG2E

    m_ref[...] = jnp.full(m_ref.shape, NEGATIVE, F32)
    for part, kv_ref in enumerate((kva_ref, kvb_ref)):

        def fold(c, _):
            here = pl.multiple_of(c * step, step)
            base = pl.multiple_of(part * half + c * step, step)
            k = kv_ref[pl.ds(here, step), :W]
            bias = bias_ref[:, pl.ds(base, step)]
            total = jnp.zeros((R, step), F32)
            for g in range(0, M, tile):
                d = nt(p_ref[g : g + tile, :W], k)
                for h in range(tile // R):
                    w = hw_ref[g + h * R : g + (h + 1) * R, :]
                    total = total + jnp.maximum(d[h * R : (h + 1) * R], 0.0) * jnp.concatenate([w] * lanes, 1)
            x_ref[:, pl.ds(base, step)] = total + bias
            lat = kv_ref[pl.ds(here, step), W:]
            for g in range(0, M, tile):
                d = nt(p_ref[g : g + tile, W:wide], lat)
                for h in range(tile // R):
                    rows = slice(g + h * R, g + (h + 1) * R)
                    s = d[h * R : (h + 1) * R] * qs + bias
                    s_ref[rows, pl.ds(base, step)] = s
                    top = m_ref[rows, :]
                    for l in range(lanes):
                        top = jnp.maximum(top, s[:, l * 128 : (l + 1) * 128])
                    m_ref[rows, :] = top
            return 0

        lax.fori_loop(0, half // step, fold, 0)

    def totals(g, _):
        rows = pl.ds(pl.multiple_of(g * 4 * R, 4 * R), 4 * R)
        top = jnp.max(m_ref[rows, :], axis=1, keepdims=True)
        topb = jnp.broadcast_to(top, (4 * R, 128))

        def inner(c, acc):
            base = pl.multiple_of(c * 512, 512)
            for l in range(4):
                acc = acc + jnp.exp2(s_ref[rows, pl.ds(base + l * 128, 128)] - topb)
            return acc

        acc = lax.fori_loop(0, S // 512, inner, jnp.zeros((4 * R, 128), F32))
        total = jnp.sum(acc, axis=1, keepdims=True)
        m_ref[rows, :] = topb + jnp.broadcast_to(jnp.log2(total), (4 * R, 128))
        return 0

    lax.fori_loop(0, heads // 4, totals, 0)

    def targets(c, _):
        base = pl.multiple_of(c * step, step)
        acc = [jnp.zeros((R, 128), F32) for _ in range(lanes)]
        for h in range(heads):
            rows = slice(h * R, (h + 1) * R)
            m = m_ref[rows, :]
            for l in range(lanes):
                acc[l] = acc[l] + jnp.exp2(s_ref[rows, pl.ds(base + l * 128, 128)] - m)
        for l in range(lanes):
            t_ref[:, pl.ds(base + l * 128, 128)] = acc[l]
        return 0

    lax.fori_loop(0, S // step, targets, 0)

    x = x_ref[...]
    e = jnp.exp(x - jnp.max(x, axis=1, keepdims=True))
    prob = e * (1.0 / jnp.sum(e, axis=1, keepdims=True))
    delta = jnp.where(bias_ref[...] == 0.0, LOSS_SCALE * (prob - t_ref[...] * (1.0 / heads)), 0.0)
    t_ref[...] = delta.astype(BF16).astype(F32)
    s_ref[:, :W] = jnp.zeros((M, W), F32)

    for part, (kv_ref, gk_ref) in enumerate(((kva_ref, gka_ref), (kvb_ref, gkb_ref))):

        def back(c, _):
            here = pl.multiple_of(c * step, step)
            base = pl.multiple_of(part * half + c * step, step)
            k = kv_ref[pl.ds(here, step), :W]
            delta = t_ref[:, pl.ds(base, step)]
            gk = jnp.zeros((W, step), F32)
            for g in range(0, M, tile):
                d = nt(p_ref[g : g + tile, :W], k)
                parts = []
                for h in range(tile // R):
                    w = hw_ref[g + h * R : g + (h + 1) * R, :]
                    parts.append(
                        jnp.where(d[h * R : (h + 1) * R] > 0.0, delta * jnp.concatenate([w] * lanes, 1), 0.0).astype(BF16)
                    )
                coef = jnp.concatenate(parts, 0)
                gk = gk + nn(iqt_ref[:, g : g + tile], coef)
                s_ref[g : g + tile, :W] += nn(coef, k)
            gk = jnp.transpose(gk).astype(BF16)
            for e in range(step // chunk):
                off = pl.multiple_of(offs_ref[c * (step // chunk) + e], chunk)
                gk_ref[pl.ds(off, chunk), :] = gk[e * chunk : (e + 1) * chunk]
            return 0

        lax.fori_loop(0, half // step, back, 0)
    gq_ref[...] = s_ref[:, :W].astype(BF16)


def shifted(sizes, axis, by):
    total = sizes[0] * sizes[1]
    pairs = []
    for i in range(total):
        a, b = divmod(i, sizes[1])
        a, b = ((a + by) % sizes[0], b) if axis == 0 else (a, (b + by) % sizes[1])
        pairs.append((i, a * sizes[1] + b))
    return pairs


def make_body(xs, zs, ys, zls):
    def body(queries, latents, index_queries, index_keys, head_weights, block_pos):
        rows = queries.shape[0]
        peers = lax.axis_size("head")
        held = queries.shape[1]
        R = rows // peers
        M = R * held * peers
        W = index_queries.shape[2]
        quarter = rows // ys
        xz = lax.axis_index("xz")
        core = lax.axis_index("core")
        head = lax.axis_index("head")
        x, z, y = xz // zs, xz % zs, head % ys

        def along_x(a, by):
            return lax.ppermute(a, "xz", shifted((xs, zs), 0, by)) if by else a

        def along_z(a, by):
            return lax.ppermute(a, "xz", shifted((xs, zs), 1, by)) if by else a

        def along_y(a, by):
            return lax.ppermute(a, "head", shifted((zls, ys), 1, by)) if by else a

        width = W + latents.shape[1]
        spare = -width % 128
        own = jnp.concatenate([index_keys, latents, jnp.zeros((rows, spare), BF16)], 1)
        piece = lax.dynamic_slice_in_dim(own, y * quarter, quarter, 0)
        from_z = jnp.concatenate([along_z(piece, d) for d in range(1, zs)], 0)
        col = jnp.concatenate([along_x(piece, d) for d in range(xs)], 0)
        hi = lax.reduce_precision(head_weights, 8, 7)
        rest = head_weights - hi
        mid = lax.reduce_precision(rest, 8, 7)
        pieces = jnp.stack([hi, mid, rest - mid], 2).astype(BF16)
        unused = jnp.zeros((rows, held, spare - 3), BF16)
        packed = jnp.concatenate([index_queries, queries, pieces, unused], 2)
        packed = jnp.transpose(packed.reshape(peers, R, held, -1), (0, 2, 1, 3))
        from_z, packed = lax.optimization_barrier((from_z, packed))
        packed = lax.all_to_all(packed, "head", split_axis=0, concat_axis=0, tiled=True).reshape(M, -1)
        row = jnp.concatenate([along_y(from_z, d) for d in range(ys)], 0)
        kva = jnp.concatenate([along_y(col, d) for d in range(ys)] + [along_x(row, d) for d in range(xs)], 0)
        kvb = lax.ppermute(kva, "core", [(0, 1), (1, 0)])

        order = [(dx, 0, dy) for dy in range(ys) for dx in range(xs)]
        order += [(dx, dz, dy) for dx in range(xs) for dy in range(ys) for dz in range(1, zs)]
        order = jnp.array(order, jnp.int32)
        ox = (x - order[:, 0]) % xs
        oz = (z - order[:, 1]) % zs
        oy = (y - order[:, 2]) % ys
        offs = (ox * zs + oz) * rows + oy * quarter
        blocks = jnp.concatenate([(ox * zs + oz) * 2 + core, (ox * zs + oz) * 2 + 1 - core])
        ids = jnp.arange(block_pos.shape[0], dtype=jnp.int32)

        def place(block):
            return jnp.sum(jnp.where(block[:, None] == ids[None, :], block_pos[None, :], 0), axis=1) * rows

        key_pos = place(blocks) + jnp.concatenate([oy, oy]) * quarter
        key_pos = (key_pos[:, None] + jnp.arange(quarter, dtype=jnp.int32)[None, :]).reshape(-1)
        query_pos = place((xz * 2 + core)[None]) + head * R + jnp.arange(R, dtype=jnp.int32)
        bias = jnp.where(key_pos[None, :] <= query_pos[:, None], 0.0, NEGATIVE).astype(F32)
        S = key_pos.shape[0]

        hw = jnp.sum(packed[:, width : width + 3].astype(F32), axis=1, keepdims=True) * (W ** (-0.5))
        hw = jnp.broadcast_to(hw, (M, 128))

        vmem = pl.BlockSpec(memory_space=pltpu.VMEM)
        gq, gka, gkb = pl.pallas_call(
            kernel,
            in_specs=[pl.BlockSpec(memory_space=pltpu.SMEM)] + [vmem] * 6,
            out_specs=(vmem, vmem, vmem),
            out_shape=(
                jax.ShapeDtypeStruct((M, W), BF16),
                jax.ShapeDtypeStruct((S // 2, W), BF16),
                jax.ShapeDtypeStruct((S // 2, W), BF16),
            ),
            scratch_shapes=[
                pltpu.VMEM((M, S), F32),
                pltpu.VMEM((M, 128), F32),
                pltpu.VMEM((R, S), F32),
                pltpu.VMEM((R, S), F32),
            ],
            compiler_params=pltpu.CompilerParams(vmem_limit_bytes=60 << 20),
            name="indexer",
        )(offs, packed, jnp.transpose(packed[:, :W]), hw, bias, kva, kvb)

        gkb = lax.ppermute(gkb, "core", [(0, 1), (1, 0)])
        gk = (gka.astype(F32) + gkb.astype(F32)).astype(BF16).reshape(xs * zs, rows, W)
        gk = lax.all_to_all(gk, "xz", split_axis=0, concat_axis=0, tiled=True)
        gk = jnp.sum(gk.astype(F32), axis=0).astype(BF16)
        last = jnp.concatenate(
            [gq.reshape(peers, M // peers, W), jnp.broadcast_to(gk[None], (peers, rows, W))], 1
        )
        last = lax.all_to_all(last, "head", split_axis=0, concat_axis=0, tiled=True)
        gq = last[:, : M // peers].reshape(peers, held, R, W)
        gq = jnp.transpose(gq, (0, 2, 1, 3)).reshape(rows, held, W).astype(F32)
        gk = jnp.sum(last[:, M // peers :].astype(F32), axis=0)
        return gq, gk

    return body


def solution(mesh):
    xs, zs, cores, zls, ys = 4, 4, 2, 2, 4
    grid = Mesh(mesh.devices.reshape(xs * zs, cores, zls * ys), ("xz", "core", "head"))
    ctx = ("xz", "core")
    return jax.shard_map(
        make_body(xs, zs, ys, zls),
        mesh=grid,
        in_specs=(
            P(ctx, "head", None),
            P(ctx, None),
            P(ctx, "head", None),
            P(ctx, None),
            P(ctx, "head"),
            P(),
        ),
        out_specs=(P(ctx, "head", None), P(ctx, None)),
        check_vma=False,
    )
```

profile of v0, /device:TPU:2, one launch (start us, length us, event | category | flops | bytes accessed | tf_op | source)
XLA Modules:
  0.0 182.3 jit_solution(4862705347167620496)
XLA Ops:
  0.7 1.1 copy.34
  1.8 0.1 pad.15.clone
  1.9 1.3 constant_dynamic-update-slice_fusion.17
  3.2 1.5 collective-permute-start.3
  4.7 2.8 %collective-permute-start.4 = (bf16[32,768]{1,0:T(8,128)(2,1)S(1)}, bf16[32,768]{1,0:T(8,128)(2,1)S(1)}, u32[]{:S(2)}, u32[]{:S(2)}) collective-permute-start(bf16[32,768]{1,0:T(8,128)(2,1)S(1)} %get-tuple-element.13), channel_id=1, source_target_pairs={{0,128},{16,144},{32,160},{48,176},{64,192},{80,208},{96,224},{112... | collective-permute-start | bytes 147464 | tf_op jit(solution)/shard_map/ppermute | solution.py:164
  7.5 0.4 collective-permute-start.5
  7.9 3.3 %collective-permute-start = (bf16[32,768]{1,0:T(8,128)(2,1)S(1)}, bf16[32,768]{1,0:T(8,128)(2,1)S(1)}, u32[]{:S(2)}, u32[]{:S(2)}) collective-permute-start(bf16[32,768]{1,0:T(8,128)(2,1)S(1)} %get-tuple-element.13), channel_id=1, source_target_pairs={{0,16},{16,32},{32,48},{48,0},{64,80},{80,96},{96,112},{112,64},{1... | collective-permute-start | bytes 147464 | tf_op jit(solution)/shard_map/ppermute | solution.py:167
  11.2 5.4 %collective-permute-start.1 = (bf16[32,768]{1,0:T(8,128)(2,1)S(1)}, bf16[32,768]{1,0:T(8,128)(2,1)S(1)}, u32[]{:S(2)}, u32[]{:S(2)}) collective-permute-start(bf16[32,768]{1,0:T(8,128)(2,1)S(1)} %get-tuple-element.13), channel_id=1, source_target_pairs={{0,32},{16,48},{32,0},{48,16},{64,96},{80,112},{96,64},{112,80},{1... | collective-permute-start | bytes 147464 | tf_op jit(solution)/shard_map/ppermute | solution.py:167
  16.6 0.7 fusion.3
  17.3 0.2 copy.36
  17.5 0.2 copy.37
  17.7 0.2 copy.38
  18.0 2.2 %copy.35 = bf16[128,8,576]{2,1,0:T(8,128)(2,1)S(1)} copy(bf16[128,8,576]{0,2,1:T(8,128)(2,1)} %param.7) | data formatting | bytes 2359296 | tf_op args[0]
  20.3 2.2 %concatenate.37 = bf16[128,8,768]{2,1,0:T(8,128)(2,1)} concatenate(bf16[128,8,128]{2,1,0:T(8,128)(2,1)S(1)} %copy-done.1, bf16[128,8,576]{2,1,0:T(8,128)(2,1)S(1)} %copy.35, bf16[128,8,1]{2,1,0:T(8,128)(2,1)S(1)} %copy.36, bf16[128,8,1]{2,1,0:T(8,128)(2,1)S(1)} %copy.37, bf16[128,8,1]{2,1,0:T(8,128)(2,1)S(1)} %copy.38, bf16[128,8,61]{2,1,0:T(8,128)(2,1)S(1)} %broadcast_in_dim.51), dimensions={2} | concatenate | bytes 3145728 | tf_op jit(solution)/shard_map/concatenate | solution.py:183
  22.4 2.7 %collective-permute-start.2 = (bf16[32,768]{1,0:T(8,128)(2,1)S(1)}, bf16[32,768]{1,0:T(8,128)(2,1)S(1)}, u32[]{:S(2)}, u32[]{:S(2)}) collective-permute-start(bf16[32,768]{1,0:T(8,128)(2,1)S(1)} %get-tuple-element.13), channel_id=1, source_target_pairs={{0,48},{16,0},{32,16},{48,32},{64,112},{80,64},{96,80},{112,96},{1... | collective-permute-start | bytes 147464 | tf_op jit(solution)/shard_map/ppermute | solution.py:167
  25.1 1.7 collective-permute-start.6
  26.8 2.9 %collective-permute-start.7 = (bf16[128,768]{1,0:T(8,128)(2,1)S(1)}, bf16[128,768]{1,0:T(8,128)(2,1)S(1)}, u32[]{:S(2)}, u32[]{:S(2)}) collective-permute-start(bf16[128,768]{1,0:T(8,128)(2,1)S(1)} %pad_maximum_fusion.1), channel_id=1, source_target_pairs={{0,2},{1,3},{2,0},{3,1},{4,6},{5,7},{6,4},{7,5},{8,10},{9,11},{10,... | collective-permute-start | bytes 589832 | tf_op jit(solution)/shard_map/ppermute | solution.py:170
  29.7 1.3 collective-permute-start.8
  31.1 0.8 collective-permute-start.9
  31.8 0.8 collective-permute-start.10
  32.6 0.6 constant_dynamic-update-slice_fusion.16
  33.2 0.6 constant_dynamic-update-slice_fusion.15
  33.9 0.6 constant_dynamic-update-slice_fusion.14
  34.5 0.8 collective-permute-done.6
  35.3 1.2 collective-permute-start.11
  36.4 0.7 constant_dynamic-update-slice_fusion.13
  37.1 2.6 %collective-permute-done.7 = bf16[128,768]{1,0:T(8,128)(2,1)S(1)} collective-permute-done((bf16[128,768]{1,0:T(8,128)(2,1)S(1)}, bf16[128,768]{1,0:T(8,128)(2,1)S(1)}, u32[]{:S(2)}, u32[]{:S(2)}) %collective-permute-start.7) | collective-permute-done | bytes 196640 | tf_op jit(solution)/shard_map/ppermute | solution.py:170
  39.8 0.7 constant_dynamic-update-slice_fusion.12
  40.4 0.7 constant_dynamic-update-slice_fusion.11
  41.1 0.7 constant_dynamic-update-slice_fusion.3
  41.8 0.7 constant_dynamic-update-slice_fusion.2
  42.5 0.7 collective-permute-done.10
  43.2 0.7 constant_dynamic-update-slice_fusion.1
  43.9 0.7 constant_dynamic-update-slice_fusion
  44.6 3.5 %collective-permute-start.13 = (bf16[384,768]{1,0:T(8,128)(2,1)S(1)}, bf16[384,768]{1,0:T(8,128)(2,1)S(1)}, u32[]{:S(2)}, u32[]{:S(2)}) collective-permute-start(bf16[384,768]{1,0:T(8,128)(2,1)S(1)} %get-tuple-element.16), channel_id=1, source_target_pairs={{0,128},{16,144},{32,160},{48,176},{64,192},{80,208},{96,224},{112... | collective-permute-start | bytes 1769480 | tf_op jit(solution)/shard_map/ppermute | solution.py:164
  48.1 12.7 %collective-permute-done.12 = bf16[384,768]{1,0:T(8,128)(2,1)S(1)} collective-permute-done((bf16[384,768]{1,0:T(8,128)(2,1)S(1)}, bf16[384,768]{1,0:T(8,128)(2,1)S(1)}, u32[]{:S(2)}, u32[]{:S(2)}) %collective-permute-start.12) | collective-permute-done | bytes 589856 | tf_op jit(solution)/shard_map/ppermute | solution.py:164
  60.8 0.9 constant_dynamic-update-slice_fusion.6
  61.7 0.6 collective-permute-done.13
  62.3 0.9 constant_dynamic-update-slice_fusion.5
  63.2 7.8 %collective-permute-done.14 = bf16[384,768]{1,0:T(8,128)(2,1)S(1)} collective-permute-done((bf16[384,768]{1,0:T(8,128)(2,1)S(1)}, bf16[384,768]{1,0:T(8,128)(2,1)S(1)}, u32[]{:S(2)}, u32[]{:S(2)}) %collective-permute-start.14) | collective-permute-done | bytes 589856 | tf_op jit(solution)/shard_map/ppermute | solution.py:164
  71.0 0.9 constant_dynamic-update-slice_fusion.4.kva_ref
  71.8 0.0 collective-permute-start.15
  71.8 3.7 %all-to-all-start = ((bf16[8,8,16,768]{3,1,2,0:T(8,128)(2,1)}), bf16[8,8,16,768]{3,1,2,0:T(8,128)(2,1)S(1)}, u32[]{:S(2)}, u32[]{:S(2)}) async-start(bf16[8,8,16,768]{3,1,2,0:T(8,128)(2,1)} %bitcast.7), calls=%async_computation | async-start | bytes 3145728 | tf_op jit(solution)/shard_map/all_to_all | solution.py:186
  75.6 0.5 add_subtract_fusion
  76.1 0.1 pad_add_fusion
  76.2 0.1 select_reduce_fusion
  76.3 0.1 fusion.16
  76.4 0.1 iota_add_fusion
  76.4 0.1 add.112
  76.5 0.6 fusion.13
  77.8 0.8 compare_select_fusion.bias_ref
  78.6 18.1 %all-to-all-done = bf16[8,8,16,768]{3,1,2,0:T(8,128)(2,1)S(1)} async-done(((bf16[8,8,16,768]{3,1,2,0:T(8,128)(2,1)}), bf16[8,8,16,768]{3,1,2,0:T(8,128)(2,1)S(1)}, u32[]{:S(2)}, u32[]{:S(2)}) %all-to-all-start) | async-done | bytes 1572896 | tf_op jit(solution)/shard_map/all_to_all | solution.py:186
  96.7 0.3 copy.39
  97.1 1.0 copy.42
  98.1 0.2 convert_reduce_fusion.1
  98.3 1.0 broadcast_in_dim.52.hw_ref
  99.3 42.9 %indexer.1 = (bf16[1024,128]{1,0:T(8,128)(2,1)}, bf16[2048,128]{1,0:T(8,128)(2,1)}, bf16[2048,128]{1,0:T(8,128)(2,1)}) custom-call(s32[64]{0:T(128)} %get-tuple-element.28.offs_ref, bf16[1024,768]{1,0:T(8,128)(2,1)} %bitcast.44, bf16[128,1024]{1,0:T(8,128)(2,1)} %bitcast.46, f32[1024,128]{1,0:T(8,128)} %broadcast_in_dim.52.hw_ref, ...), custom_call_target="tpu_custom_call" | custom-call | tf_op jit(solution)/shard_map/indexer/pallas_call | solution.py:214
  142.3 2.1 %collective-permute-done.16 = bf16[2048,128]{1,0:T(8,128)(2,1)S(1)} collective-permute-done((bf16[2048,128]{1,0:T(8,128)(2,1)}, bf16[2048,128]{1,0:T(8,128)(2,1)S(1)}, u32[]{:S(2)}, u32[]{:S(2)}) %collective-permute-start.16) | collective-permute-done | bytes 524320 | tf_op jit(solution)/shard_map/ppermute | solution.py:233
  144.4 1.2 add_convert_fusion
  145.6 23.3 %all_to_all.15 = bf16[16,128,128]{2,1,0:T(8,128)(2,1)S(1)} all-to-all(bf16[16,128,128]{2,1,0:T(8,128)(2,1)S(1)} %bitcast.45), channel_id=1, replica_groups=mesh['xz'=16,'core'=2,'head'=8] {'xz'}, dimensions={0} | all-to-all | bytes 1048576 | tf_op jit(solution)/shard_map/all_to_all | solution.py:235
  168.9 0.1 reduce_sum.51
  169.0 11.7 %all_to_all.16 = bf16[8,256,128]{2,1,0:T(8,128)(2,1)S(1)} all-to-all(bf16[8,256,128]{2,1,0:T(8,128)(2,1)S(1)} %pad_maximum_fusion), channel_id=1, replica_groups=mesh['xz'=16,'core'=2,'head'=8] {'head'}, dimensions={0} | all-to-all | bytes 1048576 | tf_op jit(solution)/shard_map/all_to_all | solution.py:240
  180.8 0.8 copy.41
  181.6 0.7 convert_reduce_fusion
  (39 shorter events, 0.3 us)
Async XLA Ops:
  0.6 19.6 %copy-start.1 = (bf16[128,8,128]{2,1,0:T(8,128)(2,1)S(1)}, bf16[128,8,128]{2,1,0:T(8,128)(2,1)}, u32[]{:S(2)}) copy-start(bf16[128,8,128]{2,1,0:T(8,128)(2,1)} %param.9) | copy-start | bytes 786436
  3.2 19.3 %collective-permute-start.3 = (bf16[32,768]{1,0:T(8,128)(2,1)S(1)}, bf16[32,768]{1,0:T(8,128)(2,1)S(1)}, u32[]{:S(2)}, u32[]{:S(2)}) collective-permute-start(bf16[32,768]{1,0:T(8,128)(2,1)S(1)} %get-tuple-element.13), channel_id=1, source_target_pairs={{0,64},{16,80},{32,96},{48,112},{64,128},{80,144},{96,160},{112,17... | collective-permute-start | bytes 147464 | tf_op jit(solution)/shard_map/ppermute | solution.py:164
  4.7 20.4 %collective-permute-start.4 = (bf16[32,768]{1,0:T(8,128)(2,1)S(1)}, bf16[32,768]{1,0:T(8,128)(2,1)S(1)}, u32[]{:S(2)}, u32[]{:S(2)}) collective-permute-start(bf16[32,768]{1,0:T(8,128)(2,1)S(1)} %get-tuple-element.13), channel_id=1, source_target_pairs={{0,128},{16,144},{32,160},{48,176},{64,192},{80,208},{96,224},{112... | collective-permute-start | bytes 147464 | tf_op jit(solution)/shard_map/ppermute | solution.py:164
  7.5 17.6 %collective-permute-start.5 = (bf16[32,768]{1,0:T(8,128)(2,1)S(1)}, bf16[32,768]{1,0:T(8,128)(2,1)S(1)}, u32[]{:S(2)}, u32[]{:S(2)}) collective-permute-start(bf16[32,768]{1,0:T(8,128)(2,1)S(1)} %get-tuple-element.13), channel_id=1, source_target_pairs={{0,192},{16,208},{32,224},{48,240},{64,0},{80,16},{96,32},{112,48}... | collective-permute-start | bytes 147464 | tf_op jit(solution)/shard_map/ppermute | solution.py:164
  7.9 21.8 %collective-permute-start = (bf16[32,768]{1,0:T(8,128)(2,1)S(1)}, bf16[32,768]{1,0:T(8,128)(2,1)S(1)}, u32[]{:S(2)}, u32[]{:S(2)}) collective-permute-start(bf16[32,768]{1,0:T(8,128)(2,1)S(1)} %get-tuple-element.13), channel_id=1, source_target_pairs={{0,16},{16,32},{32,48},{48,0},{64,80},{80,96},{96,112},{112,64},{1... | collective-permute-start | bytes 147464 | tf_op jit(solution)/shard_map/ppermute | solution.py:167
  11.2 19.8 %collective-permute-start.1 = (bf16[32,768]{1,0:T(8,128)(2,1)S(1)}, bf16[32,768]{1,0:T(8,128)(2,1)S(1)}, u32[]{:S(2)}, u32[]{:S(2)}) collective-permute-start(bf16[32,768]{1,0:T(8,128)(2,1)S(1)} %get-tuple-element.13), channel_id=1, source_target_pairs={{0,32},{16,48},{32,0},{48,16},{64,96},{80,112},{96,64},{112,80},{1... | collective-permute-start | bytes 147464 | tf_op jit(solution)/shard_map/ppermute | solution.py:167
  22.4 8.6 %collective-permute-start.2 = (bf16[32,768]{1,0:T(8,128)(2,1)S(1)}, bf16[32,768]{1,0:T(8,128)(2,1)S(1)}, u32[]{:S(2)}, u32[]{:S(2)}) collective-permute-start(bf16[32,768]{1,0:T(8,128)(2,1)S(1)} %get-tuple-element.13), channel_id=1, source_target_pairs={{0,48},{16,0},{32,16},{48,32},{64,112},{80,64},{96,80},{112,96},{1... | collective-permute-start | bytes 147464 | tf_op jit(solution)/shard_map/ppermute | solution.py:167
  25.1 10.1 %collective-permute-start.6 = (bf16[128,768]{1,0:T(8,128)(2,1)S(1)}, bf16[128,768]{1,0:T(8,128)(2,1)S(1)}, u32[]{:S(2)}, u32[]{:S(2)}) collective-permute-start(bf16[128,768]{1,0:T(8,128)(2,1)S(1)} %pad_maximum_fusion.1), channel_id=1, source_target_pairs={{0,1},{1,2},{2,3},{3,0},{4,5},{5,6},{6,7},{7,4},{8,9},{9,10},{10,1... | collective-permute-start | bytes 589832 | tf_op jit(solution)/shard_map/ppermute | solution.py:170
  26.8 13.0 %collective-permute-start.7 = (bf16[128,768]{1,0:T(8,128)(2,1)S(1)}, bf16[128,768]{1,0:T(8,128)(2,1)S(1)}, u32[]{:S(2)}, u32[]{:S(2)}) collective-permute-start(bf16[128,768]{1,0:T(8,128)(2,1)S(1)} %pad_maximum_fusion.1), channel_id=1, source_target_pairs={{0,2},{1,3},{2,0},{3,1},{4,6},{5,7},{6,4},{7,5},{8,10},{9,11},{10,... | collective-permute-start | bytes 589832 | tf_op jit(solution)/shard_map/ppermute | solution.py:170
  29.7 10.7 %collective-permute-start.8 = (bf16[128,768]{1,0:T(8,128)(2,1)S(1)}, bf16[128,768]{1,0:T(8,128)(2,1)S(1)}, u32[]{:S(2)}, u32[]{:S(2)}) collective-permute-start(bf16[128,768]{1,0:T(8,128)(2,1)S(1)} %pad_maximum_fusion.1), channel_id=1, source_target_pairs={{0,3},{1,0},{2,1},{3,2},{4,7},{5,4},{6,5},{7,6},{8,11},{9,8},{10,9... | collective-permute-start | bytes 589832 | tf_op jit(solution)/shard_map/ppermute | solution.py:170
  31.1 10.7 %collective-permute-start.9 = (bf16[96,768]{1,0:T(8,128)(2,1)S(1)}, bf16[96,768]{1,0:T(8,128)(2,1)S(1)}, u32[]{:S(2)}, u32[]{:S(2)}) collective-permute-start(bf16[96,768]{1,0:T(8,128)(2,1)S(1)} %pad_maximum_fusion.2), channel_id=1, source_target_pairs={{0,1},{1,2},{2,3},{3,0},{4,5},{5,6},{6,7},{7,4},{8,9},{9,10},{10,1... | collective-permute-start | bytes 442376 | tf_op jit(solution)/shard_map/ppermute | solution.py:170
  31.8 11.4 %collective-permute-start.10 = (bf16[96,768]{1,0:T(8,128)(2,1)S(1)}, bf16[96,768]{1,0:T(8,128)(2,1)S(1)}, u32[]{:S(2)}, u32[]{:S(2)}) collective-permute-start(bf16[96,768]{1,0:T(8,128)(2,1)S(1)} %pad_maximum_fusion.2), channel_id=1, source_target_pairs={{0,2},{1,3},{2,0},{3,1},{4,6},{5,7},{6,4},{7,5},{8,10},{9,11},{10,... | collective-permute-start | bytes 442376 | tf_op jit(solution)/shard_map/ppermute | solution.py:170
  35.3 8.6 %collective-permute-start.11 = (bf16[96,768]{1,0:T(8,128)(2,1)S(1)}, bf16[96,768]{1,0:T(8,128)(2,1)S(1)}, u32[]{:S(2)}, u32[]{:S(2)}) collective-permute-start(bf16[96,768]{1,0:T(8,128)(2,1)S(1)} %pad_maximum_fusion.2), channel_id=1, source_target_pairs={{0,3},{1,0},{2,1},{3,2},{4,7},{5,4},{6,5},{7,6},{8,11},{9,8},{10,9... | collective-permute-start | bytes 442376 | tf_op jit(solution)/shard_map/ppermute | solution.py:170
  44.6 16.2 %collective-permute-start.12 = (bf16[384,768]{1,0:T(8,128)(2,1)S(1)}, bf16[384,768]{1,0:T(8,128)(2,1)S(1)}, u32[]{:S(2)}, u32[]{:S(2)}) collective-permute-start(bf16[384,768]{1,0:T(8,128)(2,1)S(1)} %get-tuple-element.16), channel_id=1, source_target_pairs={{0,64},{16,80},{32,96},{48,112},{64,128},{80,144},{96,160},{112,17... | collective-permute-start | bytes 1769480 | tf_op jit(solution)/shard_map/ppermute | solution.py:164
  44.6 17.7 %collective-permute-start.13 = (bf16[384,768]{1,0:T(8,128)(2,1)S(1)}, bf16[384,768]{1,0:T(8,128)(2,1)S(1)}, u32[]{:S(2)}, u32[]{:S(2)}) collective-permute-start(bf16[384,768]{1,0:T(8,128)(2,1)S(1)} %get-tuple-element.16), channel_id=1, source_target_pairs={{0,128},{16,144},{32,160},{48,176},{64,192},{80,208},{96,224},{112... | collective-permute-start | bytes 1769480 | tf_op jit(solution)/shard_map/ppermute | solution.py:164
  48.1 22.9 %collective-permute-start.14 = (bf16[384,768]{1,0:T(8,128)(2,1)S(1)}, bf16[384,768]{1,0:T(8,128)(2,1)S(1)}, u32[]{:S(2)}, u32[]{:S(2)}) collective-permute-start(bf16[384,768]{1,0:T(8,128)(2,1)S(1)} %get-tuple-element.16), channel_id=1, source_target_pairs={{0,192},{16,208},{32,224},{48,240},{64,0},{80,16},{96,32},{112,48}... | collective-permute-start | bytes 1769480 | tf_op jit(solution)/shard_map/ppermute | solution.py:164
  60.8 14.7 %copy-start.3 = (s32[64,1]{0,1:T(1,128)S(1)}, s32[64,1]{0,1:T(1,128)}, u32[]{:S(2)}) copy-start(s32[64,1]{0,1:T(1,128)} %constant.95) | copy-start | bytes 772
  60.8 14.7 %copy-start.4 = (s32[64,1]{0,1:T(1,128)S(1)}, s32[64,1]{0,1:T(1,128)}, u32[]{:S(2)}) copy-start(s32[64,1]{0,1:T(1,128)} %constant.96) | copy-start | bytes 772
  60.8 14.8 %copy-start.5 = (s32[64,1]{0,1:T(1,128)S(1)}, s32[64,1]{0,1:T(1,128)}, u32[]{:S(2)}) copy-start(s32[64,1]{0,1:T(1,128)} %constant.97) | copy-start | bytes 772
  60.8 15.4 %copy-start.6 = (s32[32]{0:T(128)S(1)}, s32[32]{0:T(128)}, u32[]{:S(2)}) copy-start(s32[32]{0:T(128)} %param.12) | copy-start | bytes 388
  71.8 26.5 %collective-permute-start.15 = (bf16[2048,768]{1,0:T(8,128)(2,1)}, bf16[2048,768]{1,0:T(8,128)(2,1)}, u32[]{:S(2)}, u32[]{:S(2)}) collective-permute-start(bf16[2048,768]{1,0:T(8,128)(2,1)} %constant_dynamic-update-slice_fusion.4.kva_ref), channel_id=1, source_target_pairs={{0,8},{8,0},{1,9},{9,1},{2,10},{10,2},{3,11},{11,3},{4,12},{12,4},... | collective-permute-start | bytes 9437192 | tf_op jit(solution)/shard_map/ppermute | solution.py:189
  71.8 24.9 %all-to-all-start = ((bf16[8,8,16,768]{3,1,2,0:T(8,128)(2,1)}), bf16[8,8,16,768]{3,1,2,0:T(8,128)(2,1)S(1)}, u32[]{:S(2)}, u32[]{:S(2)}) async-start(bf16[8,8,16,768]{3,1,2,0:T(8,128)(2,1)} %bitcast.7), calls=%async_computation | async-start | bytes 3145728 | tf_op jit(solution)/shard_map/all_to_all | solution.py:186
  97.0 2.3 %copy-start = (bf16[8,8,16,768]{3,2,1,0:T(8,128)(2,1)}, bf16[8,8,16,768]{3,2,1,0:T(8,128)(2,1)S(1)}, u32[]{:S(2)}) copy-start(bf16[8,8,16,768]{3,2,1,0:T(8,128)(2,1)S(1)} %copy.39) | copy-start | bytes 4718596
  142.2 26.7 %copy-start.2 = (bf16[1024,128]{1,0:T(8,128)(2,1)S(1)}, bf16[1024,128]{1,0:T(8,128)(2,1)}, u32[]{:S(2)}) copy-start(bf16[1024,128]{1,0:T(8,128)(2,1)} %get-tuple-element.9) | copy-start | bytes 786436
  142.2 2.1 %collective-permute-start.16 = (bf16[2048,128]{1,0:T(8,128)(2,1)}, bf16[2048,128]{1,0:T(8,128)(2,1)S(1)}, u32[]{:S(2)}, u32[]{:S(2)}) collective-permute-start(bf16[2048,128]{1,0:T(8,128)(2,1)} %get-tuple-element.11), channel_id=1, source_target_pairs={{0,8},{8,0},{1,9},{9,1},{2,10},{10,2},{3,11},{11,3},{4,12},{12,4},... | collective-permute-start | bytes 1572872 | tf_op jit(solution)/shard_map/ppermute | solution.py:233
where the time goes:
time: 184 us; the launch traced here: 182 us
  waiting for transfers between devices  45.5 us (25%)
  Pallas kernels  42.9 us (23%)
  blocking collectives  35 us (19%)
  starting transfers between devices  31.9 us (17%)
  local copies, waits for them, and re-layouts  18.9 us (10%)
  other arithmetic  6.56 us (4%)
    pallas_call x1, Pallas kernels, body(): pl.pallas_call(kernel, in_specs=[pl.BlockSpec(memory_space=pltpu.SMEM)] +...  42.9 us
    all_to_all x1, blocking collectives, body(): gk = lax.all_to_all(gk, 'xz', split_axis=0, concat_axis=0, tiled=True)  23.3 us
    ppermute x6, waiting for transfers between devices, along_x(): return lax.ppermute(a, 'xz', shifted((xs, zs), 0, by)) if by else a  21.1 us
    all_to_all x1, waiting for transfers between devices, body(): lax.all_to_all(packed, 'head', split_axis=0, concat_axis=0, tiled=True)  18.1 us
    unnamed x28, local copies, waits for them, and re-layouts  12 us
    all_to_all x1, blocking collectives, body(): last = lax.all_to_all(last, 'head', split_axis=0, concat_axis=0, tiled=True)  11.7 us
    ppermute x3, starting transfers between devices, along_z(): return lax.ppermute(a, 'xz', shifted((xs, zs), 1, by)) if by else a  11.3 us
    ppermute x6, starting transfers between devices, along_y(): return lax.ppermute(a, 'head', shifted((zls, ys), 1, by)) if by else a  8.64 us
  transfers between devices with their start and end apart: 18, of which 8 were waited for; matrix products, arithmetic and copies ran while one was open for 10% of the time, Pallas kernels for 0%

commit v1 on v0

--- a/solution.py
+++ b/solution.py
@@ -25,7 +25,7 @@
     return lax.dot_general(a, b, (((1,), (0,)), ((), ())), preferred_element_type=F32)
 
 
-def kernel(offs_ref, p_ref, iqt_ref, hw_ref, bias_ref, kva_ref, kvb_ref, gq_ref, gka_ref, gkb_ref, s_ref, m_ref, x_ref, t_ref):
+def kernel(offs_ref, p_ref, iqt_ref, hw_ref, bias_ref, kva_ref, kvb_ref, gq_ref, gka_ref, gkb_ref, s_ref, m_ref, x_ref, t_ref, c_ref):
     M = p_ref.shape[0]
     R, S = bias_ref.shape
     W = iqt_ref.shape[0]
@@ -49,6 +49,7 @@
             total = jnp.zeros((R, step), F32)
             for g in range(0, M, tile):
                 d = nt(p_ref[g : g + tile, :W], k)
+                c_ref[g : g + tile, pl.ds(base, step)] = d.astype(BF16)
                 for h in range(tile // R):
                     w = hw_ref[g + h * R : g + (h + 1) * R, :]
                     total = total + jnp.maximum(d[h * R : (h + 1) * R], 0.0) * jnp.concatenate([w] * lanes, 1)
@@ -74,12 +75,12 @@
         topb = jnp.broadcast_to(top, (4 * R, 128))
 
         def inner(c, acc):
-            base = pl.multiple_of(c * 512, 512)
-            for l in range(4):
+            base = pl.multiple_of(c * 2048, 2048)
+            for l in range(16):
                 acc = acc + jnp.exp2(s_ref[rows, pl.ds(base + l * 128, 128)] - topb)
             return acc
 
-        acc = lax.fori_loop(0, S // 512, inner, jnp.zeros((4 * R, 128), F32))
+        acc = lax.fori_loop(0, S // 2048, inner, jnp.zeros((4 * R, 128), F32))
         total = jnp.sum(acc, axis=1, keepdims=True)
         m_ref[rows, :] = topb + jnp.broadcast_to(jnp.log2(total), (4 * R, 128))
         return 0
@@ -105,35 +106,41 @@
     prob = e * (1.0 / jnp.sum(e, axis=1, keepdims=True))
     delta = jnp.where(bias_ref[...] == 0.0, LOSS_SCALE * (prob - t_ref[...] * (1.0 / heads)), 0.0)
     t_ref[...] = delta.astype(BF16).astype(F32)
-    s_ref[:, :W] = jnp.zeros((M, W), F32)
-
-    for part, (kv_ref, gk_ref) in enumerate(((kva_ref, gka_ref), (kvb_ref, gkb_ref))):
-
-        def back(c, _):
-            here = pl.multiple_of(c * step, step)
-            base = pl.multiple_of(part * half + c * step, step)
-            k = kv_ref[pl.ds(here, step), :W]
-            delta = t_ref[:, pl.ds(base, step)]
-            gk = jnp.zeros((W, step), F32)
-            for g in range(0, M, tile):
-                d = nt(p_ref[g : g + tile, :W], k)
-                parts = []
-                for h in range(tile // R):
-                    w = hw_ref[g + h * R : g + (h + 1) * R, :]
-                    parts.append(
-                        jnp.where(d[h * R : (h + 1) * R] > 0.0, delta * jnp.concatenate([w] * lanes, 1), 0.0).astype(BF16)
-                    )
-                coef = jnp.concatenate(parts, 0)
-                gk = gk + nn(iqt_ref[:, g : g + tile], coef)
-                s_ref[g : g + tile, :W] += nn(coef, k)
+
+    def coefs(c, _):
+        base = pl.multiple_of(c * step, step)
+        delta = t_ref[:, pl.ds(base, step)]
+        for h in range(heads):
+            rows = slice(h * R, (h + 1) * R)
+            w = hw_ref[rows, :]
+            d = c_ref[rows, pl.ds(base, step)]
+            value = (delta * jnp.concatenate([w] * lanes, 1)).astype(BF16)
+            c_ref[rows, pl.ds(base, step)] = jnp.where(d > 0, value, jnp.zeros_like(value))
+        return 0
+
+    lax.fori_loop(0, S // step, coefs, 0)
+
+    wide_step = 4 * step
+    for part, gk_ref in enumerate((gka_ref, gkb_ref)):
+
+        def keys(c, _):
+            base = pl.multiple_of(part * half + c * wide_step, wide_step)
+            gk = nn(iqt_ref[...], c_ref[:, pl.ds(base, wide_step)])
             gk = jnp.transpose(gk).astype(BF16)
-            for e in range(step // chunk):
-                off = pl.multiple_of(offs_ref[c * (step // chunk) + e], chunk)
+            for e in range(wide_step // chunk):
+                off = pl.multiple_of(offs_ref[c * (wide_step // chunk) + e], chunk)
                 gk_ref[pl.ds(off, chunk), :] = gk[e * chunk : (e + 1) * chunk]
             return 0
 
-        lax.fori_loop(0, half // step, back, 0)
-    gq_ref[...] = s_ref[:, :W].astype(BF16)
+        lax.fori_loop(0, half // wide_step, keys, 0)
+
+    def index_queries(g, _):
+        rows = pl.ds(pl.multiple_of(g * tile, tile), tile)
+        gq = nn(c_ref[rows, :half], kva_ref[:, :W]) + nn(c_ref[rows, half:], kvb_ref[:, :W])
+        gq_ref[rows, :] = gq.astype(BF16)
+        return 0
+
+    lax.fori_loop(0, M // tile, index_queries, 0)
 
 
 def shifted(sizes, axis, by):
@@ -185,7 +192,10 @@
         from_z, packed = lax.optimization_barrier((from_z, packed))
         packed = lax.all_to_all(packed, "head", split_axis=0, concat_axis=0, tiled=True).reshape(M, -1)
         row = jnp.concatenate([along_y(from_z, d) for d in range(ys)], 0)
-        kva = jnp.concatenate([along_y(col, d) for d in range(ys)] + [along_x(row, d) for d in range(xs)], 0)
+        kva = [along_y(col, d) for d in range(ys)]
+        for d in range(xs):
+            kva.append(along_x(row, d))
+        kva = jnp.concatenate(kva, 0)
         kvb = lax.ppermute(kva, "core", [(0, 1), (1, 0)])
 
         order = [(dx, 0, dy) for dy in range(ys) for dx in range(xs)]
@@ -225,6 +235,7 @@
                 pltpu.VMEM((M, 128), F32),
                 pltpu.VMEM((R, S), F32),
                 pltpu.VMEM((R, S), F32),
+                pltpu.VMEM((M, S), BF16),
             ],
             compiler_params=pltpu.CompilerParams(vmem_limit_bytes=60 << 20),
             name="indexer",

time: 184 us -> 172 us (0.935)
  Pallas kernels: 42.9 us -> 31.2 us
    pallas_call x1, Pallas kernels: 42.9 us -> 31.2 us  [body(): pl.pallas_call(kernel, in_specs=[pl.BlockSpec(memory_space=pltpu.SMEM)] +...]
where the time goes in v1:
time: 172 us; the launch traced here: 171 us
  waiting for transfers between devices  45.5 us (26%)
  blocking collectives  35.1 us (20%)
  starting transfers between devices  31.9 us (19%)
  Pallas kernels  31.2 us (18%)
  local copies, waits for them, and re-layouts  18.9 us (11%)
  other arithmetic  6.56 us (4%)
    pallas_call x1, Pallas kernels, body(): pl.pallas_call(kernel, in_specs=[pl.BlockSpec(memory_space=pltpu.SMEM)] +...  31.2 us
    all_to_all x1, blocking collectives, body(): gk = lax.all_to_all(gk, 'xz', split_axis=0, concat_axis=0, tiled=True)  23.3 us
    ppermute x6, waiting for transfers between devices, along_x(): return lax.ppermute(a, 'xz', shifted((xs, zs), 0, by)) if by else a  21.1 us
    all_to_all x1, waiting for transfers between devices, body(): lax.all_to_all(packed, 'head', split_axis=0, concat_axis=0, tiled=True)  18.1 us
    unnamed x28, local copies, waits for them, and re-layouts  12 us
    all_to_all x1, blocking collectives, body(): last = lax.all_to_all(last, 'head', split_axis=0, concat_axis=0, tiled=True)  11.7 us
    ppermute x3, starting transfers between devices, along_z(): return lax.ppermute(a, 'xz', shifted((xs, zs), 1, by)) if by else a  11.3 us
    ppermute x6, starting transfers between devices, along_y(): return lax.ppermute(a, 'head', shifted((zls, ys), 1, by)) if by else a  8.64 us
  transfers between devices with their start and end apart: 18, of which 8 were waited for; matrix products, arithmetic and copies ran while one was open for 10% of the time, Pallas kernels for 0%

profile of v1, /device:TPU:2, one launch (start us, length us, event | category | flops | bytes accessed | tf_op | source)
XLA Modules:
  0.0 170.6 jit_solution(15064786065344283538)
XLA Ops:
  0.7 1.1 copy.34
  1.8 0.1 pad.15.clone
  1.9 1.3 constant_dynamic-update-slice_fusion.17
  3.2 1.5 collective-permute-start.3
  4.7 2.8 %collective-permute-start.4 = (bf16[32,768]{1,0:T(8,128)(2,1)S(1)}, bf16[32,768]{1,0:T(8,128)(2,1)S(1)}, u32[]{:S(2)}, u32[]{:S(2)}) collective-permute-start(bf16[32,768]{1,0:T(8,128)(2,1)S(1)} %get-tuple-element.13), channel_id=1, source_target_pairs={{0,128},{16,144},{32,160},{48,176},{64,192},{80,208},{96,224},{112... | collective-permute-start | bytes 147464 | tf_op jit(solution)/shard_map/ppermute | solution.py:171
  7.5 0.4 collective-permute-start.5
  7.9 3.3 %collective-permute-start = (bf16[32,768]{1,0:T(8,128)(2,1)S(1)}, bf16[32,768]{1,0:T(8,128)(2,1)S(1)}, u32[]{:S(2)}, u32[]{:S(2)}) collective-permute-start(bf16[32,768]{1,0:T(8,128)(2,1)S(1)} %get-tuple-element.13), channel_id=1, source_target_pairs={{0,16},{16,32},{32,48},{48,0},{64,80},{80,96},{96,112},{112,64},{1... | collective-permute-start | bytes 147464 | tf_op jit(solution)/shard_map/ppermute | solution.py:174
  11.2 5.4 %collective-permute-start.1 = (bf16[32,768]{1,0:T(8,128)(2,1)S(1)}, bf16[32,768]{1,0:T(8,128)(2,1)S(1)}, u32[]{:S(2)}, u32[]{:S(2)}) collective-permute-start(bf16[32,768]{1,0:T(8,128)(2,1)S(1)} %get-tuple-element.13), channel_id=1, source_target_pairs={{0,32},{16,48},{32,0},{48,16},{64,96},{80,112},{96,64},{112,80},{1... | collective-permute-start | bytes 147464 | tf_op jit(solution)/shard_map/ppermute | solution.py:174
  16.6 0.7 fusion.3
  17.3 0.2 copy.36
  17.5 0.2 copy.37
  17.7 0.2 copy.38
  18.0 2.2 %copy.35 = bf16[128,8,576]{2,1,0:T(8,128)(2,1)S(1)} copy(bf16[128,8,576]{0,2,1:T(8,128)(2,1)} %param.7) | data formatting | bytes 2359296 | tf_op args[0]
  20.3 2.2 %concatenate.37 = bf16[128,8,768]{2,1,0:T(8,128)(2,1)} concatenate(bf16[128,8,128]{2,1,0:T(8,128)(2,1)S(1)} %copy-done.1, bf16[128,8,576]{2,1,0:T(8,128)(2,1)S(1)} %copy.35, bf16[128,8,1]{2,1,0:T(8,128)(2,1)S(1)} %copy.36, bf16[128,8,1]{2,1,0:T(8,128)(2,1)S(1)} %copy.37, bf16[128,8,1]{2,1,0:T(8,128)(2,1)S(1)} %copy.38, bf16[128,8,61]{2,1,0:T(8,128)(2,1)S(1)} %broadcast_in_dim.51), dimensions={2} | concatenate | bytes 3145728 | tf_op jit(solution)/shard_map/concatenate | solution.py:190
  22.4 2.7 %collective-permute-start.2 = (bf16[32,768]{1,0:T(8,128)(2,1)S(1)}, bf16[32,768]{1,0:T(8,128)(2,1)S(1)}, u32[]{:S(2)}, u32[]{:S(2)}) collective-permute-start(bf16[32,768]{1,0:T(8,128)(2,1)S(1)} %get-tuple-element.13), channel_id=1, source_target_pairs={{0,48},{16,0},{32,16},{48,32},{64,112},{80,64},{96,80},{112,96},{1... | collective-permute-start | bytes 147464 | tf_op jit(solution)/shard_map/ppermute | solution.py:174
  25.1 1.7 collective-permute-start.6
  26.8 2.9 %collective-permute-start.7 = (bf16[128,768]{1,0:T(8,128)(2,1)S(1)}, bf16[128,768]{1,0:T(8,128)(2,1)S(1)}, u32[]{:S(2)}, u32[]{:S(2)}) collective-permute-start(bf16[128,768]{1,0:T(8,128)(2,1)S(1)} %pad_maximum_fusion.1), channel_id=1, source_target_pairs={{0,2},{1,3},{2,0},{3,1},{4,6},{5,7},{6,4},{7,5},{8,10},{9,11},{10,... | collective-permute-start | bytes 589832 | tf_op jit(solution)/shard_map/ppermute | solution.py:177
  29.7 1.3 collective-permute-start.8
  31.1 0.8 collective-permute-start.9
  31.8 0.8 collective-permute-start.10
  32.6 0.6 constant_dynamic-update-slice_fusion.16
  33.2 0.6 constant_dynamic-update-slice_fusion.15
  33.9 0.6 constant_dynamic-update-slice_fusion.14
  34.5 0.8 collective-permute-done.6
  35.3 1.2 collective-permute-start.11
  36.4 0.7 constant_dynamic-update-slice_fusion.13
  37.1 2.6 %collective-permute-done.7 = bf16[128,768]{1,0:T(8,128)(2,1)S(1)} collective-permute-done((bf16[128,768]{1,0:T(8,128)(2,1)S(1)}, bf16[128,768]{1,0:T(8,128)(2,1)S(1)}, u32[]{:S(2)}, u32[]{:S(2)}) %collective-permute-start.7) | collective-permute-done | bytes 196640 | tf_op jit(solution)/shard_map/ppermute | solution.py:177
  39.8 0.7 constant_dynamic-update-slice_fusion.12
  40.4 0.7 constant_dynamic-update-slice_fusion.11
  41.1 0.7 constant_dynamic-update-slice_fusion.3
  41.8 0.7 constant_dynamic-update-slice_fusion.2
  42.5 0.7 collective-permute-done.10
  43.2 0.7 constant_dynamic-update-slice_fusion.1
  43.9 0.7 constant_dynamic-update-slice_fusion
  44.6 3.5 %collective-permute-start.13 = (bf16[384,768]{1,0:T(8,128)(2,1)S(1)}, bf16[384,768]{1,0:T(8,128)(2,1)S(1)}, u32[]{:S(2)}, u32[]{:S(2)}) collective-permute-start(bf16[384,768]{1,0:T(8,128)(2,1)S(1)} %get-tuple-element.16), channel_id=1, source_target_pairs={{0,128},{16,144},{32,160},{48,176},{64,192},{80,208},{96,224},{112... | collective-permute-start | bytes 1769480 | tf_op jit(solution)/shard_map/ppermute | solution.py:171
  48.1 12.7 %collective-permute-done.12 = bf16[384,768]{1,0:T(8,128)(2,1)S(1)} collective-permute-done((bf16[384,768]{1,0:T(8,128)(2,1)S(1)}, bf16[384,768]{1,0:T(8,128)(2,1)S(1)}, u32[]{:S(2)}, u32[]{:S(2)}) %collective-permute-start.12) | collective-permute-done | bytes 589856 | tf_op jit(solution)/shard_map/ppermute | solution.py:171
  60.8 0.9 constant_dynamic-update-slice_fusion.6
  61.7 0.6 collective-permute-done.13
  62.3 0.9 constant_dynamic-update-slice_fusion.5
  63.2 7.8 %collective-permute-done.14 = bf16[384,768]{1,0:T(8,128)(2,1)S(1)} collective-permute-done((bf16[384,768]{1,0:T(8,128)(2,1)S(1)}, bf16[384,768]{1,0:T(8,128)(2,1)S(1)}, u32[]{:S(2)}, u32[]{:S(2)}) %collective-permute-start.14) | collective-permute-done | bytes 589856 | tf_op jit(solution)/shard_map/ppermute | solution.py:171
  71.0 0.9 constant_dynamic-update-slice_fusion.4.kva_ref
  71.8 0.0 collective-permute-start.15
  71.8 3.7 %all-to-all-start = ((bf16[8,8,16,768]{3,1,2,0:T(8,128)(2,1)}), bf16[8,8,16,768]{3,1,2,0:T(8,128)(2,1)S(1)}, u32[]{:S(2)}, u32[]{:S(2)}) async-start(bf16[8,8,16,768]{3,1,2,0:T(8,128)(2,1)} %bitcast.7), calls=%async_computation | async-start | bytes 3145728 | tf_op jit(solution)/shard_map/all_to_all | solution.py:193
  75.6 0.5 add_subtract_fusion
  76.1 0.1 pad_add_fusion
  76.2 0.1 select_reduce_fusion
  76.3 0.1 fusion.16
  76.4 0.1 iota_add_fusion
  76.4 0.1 add.112
  76.5 0.6 fusion.13
  77.8 0.8 compare_select_fusion.bias_ref
  78.6 18.1 %all-to-all-done = bf16[8,8,16,768]{3,1,2,0:T(8,128)(2,1)S(1)} async-done(((bf16[8,8,16,768]{3,1,2,0:T(8,128)(2,1)}), bf16[8,8,16,768]{3,1,2,0:T(8,128)(2,1)S(1)}, u32[]{:S(2)}, u32[]{:S(2)}) %all-to-all-start) | async-done | bytes 1572896 | tf_op jit(solution)/shard_map/all_to_all | solution.py:193
  96.7 0.3 copy.39
  97.1 1.0 copy.42
  98.1 0.2 convert_reduce_fusion.1
  98.3 1.0 broadcast_in_dim.52.hw_ref
  99.3 31.2 %indexer.1 = (bf16[1024,128]{1,0:T(8,128)(2,1)}, bf16[2048,128]{1,0:T(8,128)(2,1)}, bf16[2048,128]{1,0:T(8,128)(2,1)}) custom-call(s32[64]{0:T(128)} %get-tuple-element.28.offs_ref, bf16[1024,768]{1,0:T(8,128)(2,1)} %bitcast.44, bf16[128,1024]{1,0:T(8,128)(2,1)} %bitcast.46, f32[1024,128]{1,0:T(8,128)} %broadcast_in_dim.52.hw_ref, ...), custom_call_target="tpu_custom_call" | custom-call | tf_op jit(solution)/shard_map/indexer/pallas_call | solution.py:224
  130.5 2.1 %collective-permute-done.16 = bf16[2048,128]{1,0:T(8,128)(2,1)S(1)} collective-permute-done((bf16[2048,128]{1,0:T(8,128)(2,1)}, bf16[2048,128]{1,0:T(8,128)(2,1)S(1)}, u32[]{:S(2)}, u32[]{:S(2)}) %collective-permute-start.16) | collective-permute-done | bytes 524320 | tf_op jit(solution)/shard_map/ppermute | solution.py:244
  132.7 1.2 add_convert_fusion
  133.8 23.3 %all_to_all.15 = bf16[16,128,128]{2,1,0:T(8,128)(2,1)S(1)} all-to-all(bf16[16,128,128]{2,1,0:T(8,128)(2,1)S(1)} %bitcast.45), channel_id=1, replica_groups=mesh['xz'=16,'core'=2,'head'=8] {'xz'}, dimensions={0} | all-to-all | bytes 1048576 | tf_op jit(solution)/shard_map/all_to_all | solution.py:246
  157.1 0.1 reduce_sum.51
  157.3 11.7 %all_to_all.16 = bf16[8,256,128]{2,1,0:T(8,128)(2,1)S(1)} all-to-all(bf16[8,256,128]{2,1,0:T(8,128)(2,1)S(1)} %pad_maximum_fusion), channel_id=1, replica_groups=mesh['xz'=16,'core'=2,'head'=8] {'head'}, dimensions={0} | all-to-all | bytes 1048576 | tf_op jit(solution)/shard_map/all_to_all | solution.py:251
  169.1 0.8 copy.41
  169.9 0.7 convert_reduce_fusion
  (39 shorter events, 0.3 us)
Async XLA Ops:
  0.6 19.6 %copy-start.1 = (bf16[128,8,128]{2,1,0:T(8,128)(2,1)S(1)}, bf16[128,8,128]{2,1,0:T(8,128)(2,1)}, u32[]{:S(2)}) copy-start(bf16[128,8,128]{2,1,0:T(8,128)(2,1)} %param.9) | copy-start | bytes 786436
  3.2 19.3 %collective-permute-start.3 = (bf16[32,768]{1,0:T(8,128)(2,1)S(1)}, bf16[32,768]{1,0:T(8,128)(2,1)S(1)}, u32[]{:S(2)}, u32[]{:S(2)}) collective-permute-start(bf16[32,768]{1,0:T(8,128)(2,1)S(1)} %get-tuple-element.13), channel_id=1, source_target_pairs={{0,64},{16,80},{32,96},{48,112},{64,128},{80,144},{96,160},{112,17... | collective-permute-start | bytes 147464 | tf_op jit(solution)/shard_map/ppermute | solution.py:171
  4.7 20.4 %collective-permute-start.4 = (bf16[32,768]{1,0:T(8,128)(2,1)S(1)}, bf16[32,768]{1,0:T(8,128)(2,1)S(1)}, u32[]{:S(2)}, u32[]{:S(2)}) collective-permute-start(bf16[32,768]{1,0:T(8,128)(2,1)S(1)} %get-tuple-element.13), channel_id=1, source_target_pairs={{0,128},{16,144},{32,160},{48,176},{64,192},{80,208},{96,224},{112... | collective-permute-start | bytes 147464 | tf_op jit(solution)/shard_map/ppermute | solution.py:171
  7.5 17.6 %collective-permute-start.5 = (bf16[32,768]{1,0:T(8,128)(2,1)S(1)}, bf16[32,768]{1,0:T(8,128)(2,1)S(1)}, u32[]{:S(2)}, u32[]{:S(2)}) collective-permute-start(bf16[32,768]{1,0:T(8,128)(2,1)S(1)} %get-tuple-element.13), channel_id=1, source_target_pairs={{0,192},{16,208},{32,224},{48,240},{64,0},{80,16},{96,32},{112,48}... | collective-permute-start | bytes 147464 | tf_op jit(solution)/shard_map/ppermute | solution.py:171
  7.9 21.8 %collective-permute-start = (bf16[32,768]{1,0:T(8,128)(2,1)S(1)}, bf16[32,768]{1,0:T(8,128)(2,1)S(1)}, u32[]{:S(2)}, u32[]{:S(2)}) collective-permute-start(bf16[32,768]{1,0:T(8,128)(2,1)S(1)} %get-tuple-element.13), channel_id=1, source_target_pairs={{0,16},{16,32},{32,48},{48,0},{64,80},{80,96},{96,112},{112,64},{1... | collective-permute-start | bytes 147464 | tf_op jit(solution)/shard_map/ppermute | solution.py:174
  11.2 19.8 %collective-permute-start.1 = (bf16[32,768]{1,0:T(8,128)(2,1)S(1)}, bf16[32,768]{1,0:T(8,128)(2,1)S(1)}, u32[]{:S(2)}, u32[]{:S(2)}) collective-permute-start(bf16[32,768]{1,0:T(8,128)(2,1)S(1)} %get-tuple-element.13), channel_id=1, source_target_pairs={{0,32},{16,48},{32,0},{48,16},{64,96},{80,112},{96,64},{112,80},{1... | collective-permute-start | bytes 147464 | tf_op jit(solution)/shard_map/ppermute | solution.py:174
  22.4 8.6 %collective-permute-start.2 = (bf16[32,768]{1,0:T(8,128)(2,1)S(1)}, bf16[32,768]{1,0:T(8,128)(2,1)S(1)}, u32[]{:S(2)}, u32[]{:S(2)}) collective-permute-start(bf16[32,768]{1,0:T(8,128)(2,1)S(1)} %get-tuple-element.13), channel_id=1, source_target_pairs={{0,48},{16,0},{32,16},{48,32},{64,112},{80,64},{96,80},{112,96},{1... | collective-permute-start | bytes 147464 | tf_op jit(solution)/shard_map/ppermute | solution.py:174
  25.1 10.1 %collective-permute-start.6 = (bf16[128,768]{1,0:T(8,128)(2,1)S(1)}, bf16[128,768]{1,0:T(8,128)(2,1)S(1)}, u32[]{:S(2)}, u32[]{:S(2)}) collective-permute-start(bf16[128,768]{1,0:T(8,128)(2,1)S(1)} %pad_maximum_fusion.1), channel_id=1, source_target_pairs={{0,1},{1,2},{2,3},{3,0},{4,5},{5,6},{6,7},{7,4},{8,9},{9,10},{10,1... | collective-permute-start | bytes 589832 | tf_op jit(solution)/shard_map/ppermute | solution.py:177
  26.8 13.0 %collective-permute-start.7 = (bf16[128,768]{1,0:T(8,128)(2,1)S(1)}, bf16[128,768]{1,0:T(8,128)(2,1)S(1)}, u32[]{:S(2)}, u32[]{:S(2)}) collective-permute-start(bf16[128,768]{1,0:T(8,128)(2,1)S(1)} %pad_maximum_fusion.1), channel_id=1, source_target_pairs={{0,2},{1,3},{2,0},{3,1},{4,6},{5,7},{6,4},{7,5},{8,10},{9,11},{10,... | collective-permute-start | bytes 589832 | tf_op jit(solution)/shard_map/ppermute | solution.py:177
  29.7 10.7 %collective-permute-start.8 = (bf16[128,768]{1,0:T(8,128)(2,1)S(1)}, bf16[128,768]{1,0:T(8,128)(2,1)S(1)}, u32[]{:S(2)}, u32[]{:S(2)}) collective-permute-start(bf16[128,768]{1,0:T(8,128)(2,1)S(1)} %pad_maximum_fusion.1), channel_id=1, source_target_pairs={{0,3},{1,0},{2,1},{3,2},{4,7},{5,4},{6,5},{7,6},{8,11},{9,8},{10,9... | collective-permute-start | bytes 589832 | tf_op jit(solution)/shard_map/ppermute | solution.py:177
  31.1 10.7 %collective-permute-start.9 = (bf16[96,768]{1,0:T(8,128)(2,1)S(1)}, bf16[96,768]{1,0:T(8,128)(2,1)S(1)}, u32[]{:S(2)}, u32[]{:S(2)}) collective-permute-start(bf16[96,768]{1,0:T(8,128)(2,1)S(1)} %pad_maximum_fusion.2), channel_id=1, source_target_pairs={{0,1},{1,2},{2,3},{3,0},{4,5},{5,6},{6,7},{7,4},{8,9},{9,10},{10,1... | collective-permute-start | bytes 442376 | tf_op jit(solution)/shard_map/ppermute | solution.py:177
  31.8 11.4 %collective-permute-start.10 = (bf16[96,768]{1,0:T(8,128)(2,1)S(1)}, bf16[96,768]{1,0:T(8,128)(2,1)S(1)}, u32[]{:S(2)}, u32[]{:S(2)}) collective-permute-start(bf16[96,768]{1,0:T(8,128)(2,1)S(1)} %pad_maximum_fusion.2), channel_id=1, source_target_pairs={{0,2},{1,3},{2,0},{3,1},{4,6},{5,7},{6,4},{7,5},{8,10},{9,11},{10,... | collective-permute-start | bytes 442376 | tf_op jit(solution)/shard_map/ppermute | solution.py:177
  35.3 8.6 %collective-permute-start.11 = (bf16[96,768]{1,0:T(8,128)(2,1)S(1)}, bf16[96,768]{1,0:T(8,128)(2,1)S(1)}, u32[]{:S(2)}, u32[]{:S(2)}) collective-permute-start(bf16[96,768]{1,0:T(8,128)(2,1)S(1)} %pad_maximum_fusion.2), channel_id=1, source_target_pairs={{0,3},{1,0},{2,1},{3,2},{4,7},{5,4},{6,5},{7,6},{8,11},{9,8},{10,9... | collective-permute-start | bytes 442376 | tf_op jit(solution)/shard_map/ppermute | solution.py:177
  44.6 16.2 %collective-permute-start.12 = (bf16[384,768]{1,0:T(8,128)(2,1)S(1)}, bf16[384,768]{1,0:T(8,128)(2,1)S(1)}, u32[]{:S(2)}, u32[]{:S(2)}) collective-permute-start(bf16[384,768]{1,0:T(8,128)(2,1)S(1)} %get-tuple-element.16), channel_id=1, source_target_pairs={{0,64},{16,80},{32,96},{48,112},{64,128},{80,144},{96,160},{112,17... | collective-permute-start | bytes 1769480 | tf_op jit(solution)/shard_map/ppermute | solution.py:171
  44.6 17.7 %collective-permute-start.13 = (bf16[384,768]{1,0:T(8,128)(2,1)S(1)}, bf16[384,768]{1,0:T(8,128)(2,1)S(1)}, u32[]{:S(2)}, u32[]{:S(2)}) collective-permute-start(bf16[384,768]{1,0:T(8,128)(2,1)S(1)} %get-tuple-element.16), channel_id=1, source_target_pairs={{0,128},{16,144},{32,160},{48,176},{64,192},{80,208},{96,224},{112... | collective-permute-start | bytes 1769480 | tf_op jit(solution)/shard_map/ppermute | solution.py:171
  48.1 22.9 %collective-permute-start.14 = (bf16[384,768]{1,0:T(8,128)(2,1)S(1)}, bf16[384,768]{1,0:T(8,128)(2,1)S(1)}, u32[]{:S(2)}, u32[]{:S(2)}) collective-permute-start(bf16[384,768]{1,0:T(8,128)(2,1)S(1)} %get-tuple-element.16), channel_id=1, source_target_pairs={{0,192},{16,208},{32,224},{48,240},{64,0},{80,16},{96,32},{112,48}... | collective-permute-start | bytes 1769480 | tf_op jit(solution)/shard_map/ppermute | solution.py:171
  60.8 14.7 %copy-start.3 = (s32[64,1]{0,1:T(1,128)S(1)}, s32[64,1]{0,1:T(1,128)}, u32[]{:S(2)}) copy-start(s32[64,1]{0,1:T(1,128)} %constant.95) | copy-start | bytes 772
  60.8 14.7 %copy-start.4 = (s32[64,1]{0,1:T(1,128)S(1)}, s32[64,1]{0,1:T(1,128)}, u32[]{:S(2)}) copy-start(s32[64,1]{0,1:T(1,128)} %constant.96) | copy-start | bytes 772
  60.8 14.8 %copy-start.5 = (s32[64,1]{0,1:T(1,128)S(1)}, s32[64,1]{0,1:T(1,128)}, u32[]{:S(2)}) copy-start(s32[64,1]{0,1:T(1,128)} %constant.97) | copy-start | bytes 772
  60.8 15.4 %copy-start.6 = (s32[32]{0:T(128)S(1)}, s32[32]{0:T(128)}, u32[]{:S(2)}) copy-start(s32[32]{0:T(128)} %param.12) | copy-start | bytes 388
  71.8 26.5 %collective-permute-start.15 = (bf16[2048,768]{1,0:T(8,128)(2,1)}, bf16[2048,768]{1,0:T(8,128)(2,1)}, u32[]{:S(2)}, u32[]{:S(2)}) collective-permute-start(bf16[2048,768]{1,0:T(8,128)(2,1)} %constant_dynamic-update-slice_fusion.4.kva_ref), channel_id=1, source_target_pairs={{0,8},{8,0},{1,9},{9,1},{2,10},{10,2},{3,11},{11,3},{4,12},{12,4},... | collective-permute-start | bytes 9437192 | tf_op jit(solution)/shard_map/ppermute | solution.py:199
  71.8 24.9 %all-to-all-start = ((bf16[8,8,16,768]{3,1,2,0:T(8,128)(2,1)}), bf16[8,8,16,768]{3,1,2,0:T(8,128)(2,1)S(1)}, u32[]{:S(2)}, u32[]{:S(2)}) async-start(bf16[8,8,16,768]{3,1,2,0:T(8,128)(2,1)} %bitcast.7), calls=%async_computation | async-start | bytes 3145728 | tf_op jit(solution)/shard_map/all_to_all | solution.py:193
  97.0 2.3 %copy-start = (bf16[8,8,16,768]{3,2,1,0:T(8,128)(2,1)}, bf16[8,8,16,768]{3,2,1,0:T(8,128)(2,1)S(1)}, u32[]{:S(2)}) copy-start(bf16[8,8,16,768]{3,2,1,0:T(8,128)(2,1)S(1)} %copy.39) | copy-start | bytes 4718596
  130.5 26.7 %copy-start.2 = (bf16[1024,128]{1,0:T(8,128)(2,1)S(1)}, bf16[1024,128]{1,0:T(8,128)(2,1)}, u32[]{:S(2)}) copy-start(bf16[1024,128]{1,0:T(8,128)(2,1)} %get-tuple-element.9) | copy-start | bytes 786436
  130.5 2.1 %collective-permute-start.16 = (bf16[2048,128]{1,0:T(8,128)(2,1)}, bf16[2048,128]{1,0:T(8,128)(2,1)S(1)}, u32[]{:S(2)}, u32[]{:S(2)}) collective-permute-start(bf16[2048,128]{1,0:T(8,128)(2,1)} %get-tuple-element.11), channel_id=1, source_target_pairs={{0,8},{8,0},{1,9},{9,1},{2,10},{10,2},{3,11},{11,3},{4,12},{12,4},... | collective-permute-start | bytes 1572872 | tf_op jit(solution)/shard_map/ppermute | solution.py:244
